TPU v7x, 32 devices: a whole 2x2x4 slice. The times are simulated.
32 devices in a mesh: replica: 2 (over x), pipe: 4 (over z), tensor: 4 (over y, core).
Axes of the slice: x: 2, y: 2, z: 4, core: 2. Of those that a mesh axis runs over, the one named last changes fastest.
Arguments:
- queries: bfloat16 [256, 8192], P('replica', ('pipe', 'tensor')), parts along dimension 0, may hold values from -128 to 128, as said below
- cache_keys: bfloat16 [8, 4096, 1024], P('replica', 'tensor', 'pipe'), parts along dimension 0, may hold values from -4 to 4
- cache_values: bfloat16 [8, 4096, 1024], P('replica', 'tensor', 'pipe'), parts along dimension 0, may hold values from -6 to 6
- prefix_lengths: int32 [8], P('replica'), parts along dimension 0, may hold values from 2048 to 4064
- residual_in: bfloat16 [256, 8192], P('replica', ('pipe', 'tensor')), parts along dimension 0, may hold values from -64 to 64
- out_weight: bfloat16 [8192, 4, 2048], P('pipe', None, 'tensor'), may hold values from -0.0625 to 0.0625
- norm_gain: float32 [8192], P(('pipe', 'tensor')), may hold values from 0.1 to 1.9
Outputs:
- residual_out: bfloat16 [256, 8192], P('replica', ('pipe', 'tensor')), parts along dimension 0
- normed: bfloat16 [256, 8192], P('replica', ('pipe', 'tensor')), parts along dimension 0
There are 2 independent parts, one for each index of `replica`. A program takes and returns all parts, laid end to end along the dimension named above; an argument that names none is the same for every part. Nothing has to cross between parts.
Inputs may be any that keep to these rules, and one draw needn't show every extreme that they name: `queries`: entries of the query rows; some rows may be much longer than others. The span's own keys and values already stand in the cache, in slots prefix_lengths[r] to prefix_lengths[r] + 31; later slots hold unused entries.
All inputs are finite; a program needn't handle non-finite values.
Results may differ from a plain program's by a relative error of at most 0.018.
Values may be sent and summed in bfloat16 or wider, within the bound.
A program may use at most 64 MiB of HBM per device.

v0:
```python
import math
import jax
import jax.numpy as jnp
from jax import lax
from jax.sharding import PartitionSpec as P

D = 8192
HD = 128
masked_value = -1e30
epsilon = 1e-05


def combined_all(shard, axis, combine):
    everything = jax.tree.map(
        lambda part, kind: lax.all_gather(part.astype(kind), axis),
        shard,
        (jnp.bfloat16, jnp.bfloat16, jnp.bfloat16),
    )

    def take(k):
        return jax.tree.map(lambda part, own: part[k].astype(own.dtype), everything, shard)

    return lax.fori_loop(
        1, lax.axis_size(axis), lambda k, so_far: combine(so_far, take(k)), take(0)
    )


def combine(first, second):
    peak_one, total_one, summed_one = first
    peak_two, total_two, summed_two = second
    joined = jnp.maximum(peak_one, peak_two)
    factor_one = jnp.exp(peak_one - joined)
    factor_two = jnp.exp(peak_two - joined)
    return (
        joined,
        total_one * factor_one + total_two * factor_two,
        summed_one * factor_one[..., None] + summed_two * factor_two[..., None],
    )


def on_device(
    queries, cache_keys, cache_values, prefix_lengths, residual_in, out_weight, norm_gain
):
    tok_rows = queries.shape[0]
    requests = prefix_lengths.shape[0]
    span_len = tok_rows // requests
    slot_count = cache_keys.shape[1]
    local_groups = cache_keys.shape[2] // HD
    gathered = lax.all_gather(queries, "tensor", axis=1, tiled=True)
    heads_here = gathered.shape[1] // HD
    group_size = heads_here // local_groups
    queries_here = gathered.reshape(requests, span_len, local_groups, group_size, HD)
    keys_here = cache_keys.reshape(requests, slot_count, local_groups, HD)
    values_here = cache_values.reshape(requests, slot_count, local_groups, HD)
    scores = jnp.einsum(
        "rcghd,rjgd->rcghj", queries_here, keys_here, preferred_element_type=jnp.float32
    ) * (1.0 / math.sqrt(HD))
    first_slot = lax.axis_index("tensor") * slot_count
    slot_index = first_slot + jnp.arange(slot_count, dtype=jnp.int32)
    limits = prefix_lengths[:, None] + jnp.arange(span_len, dtype=jnp.int32)[None, :]
    visible = (slot_index[None, None, :] <= limits[:, :, None])[:, :, None, None, :]
    masked = jnp.where(visible, scores, masked_value)
    row_peak = jnp.max(masked, axis=-1)
    weights = jnp.where(visible, jnp.exp(masked - row_peak[..., None]), 0.0)
    row_total = jnp.sum(weights, axis=-1)
    weighted = jnp.einsum(
        "rcghj,rjgd->rcghd",
        weights.astype(jnp.bfloat16),
        values_here,
        preferred_element_type=jnp.float32,
    )
    row_peak = row_peak.reshape(tok_rows, heads_here)
    row_total = row_total.reshape(tok_rows, heads_here)
    weighted = weighted.reshape(tok_rows, heads_here, HD)
    row_peak, row_total, weighted = combined_all((row_peak, row_total, weighted), "tensor", combine)
    attended = (
        (weighted / row_total[..., None]).astype(jnp.bfloat16).reshape(tok_rows, heads_here * HD)
    )
    col_groups = out_weight.shape[1]
    col_width = out_weight.shape[2]
    partial_value = jnp.dot(
        attended,
        out_weight.reshape(out_weight.shape[0], col_groups * col_width),
        preferred_element_type=jnp.float32,
    )
    projected = (
        lax.psum_scatter(
            partial_value.reshape(tok_rows, col_groups, col_width).astype(jnp.bfloat16),
            "pipe",
            scatter_dimension=1,
            tiled=True,
        )
        .astype(jnp.float32)
        .reshape(tok_rows, col_width)
    )
    updated = residual_in.astype(jnp.float32) + projected
    squares = lax.psum(jnp.sum(updated * updated, axis=1), ("pipe", "tensor"))
    normed = updated * lax.rsqrt(squares / D + epsilon)[:, None] * norm_gain[None, :]
    return (updated.astype(jnp.bfloat16), normed.astype(jnp.bfloat16))


def solution(mesh):
    in_specs = (
        P("replica", ("pipe", "tensor")),
        P("replica", "tensor", "pipe"),
        P("replica", "tensor", "pipe"),
        P("replica"),
        P("replica", ("pipe", "tensor")),
        P("pipe", None, "tensor"),
        P(("pipe", "tensor")),
    )
    out_specs = (P("replica", ("pipe", "tensor")), P("replica", ("pipe", "tensor")))
    return jax.shard_map(
        on_device, mesh=mesh, in_specs=in_specs, out_specs=out_specs, check_vma=False
    )
```

profile of v0, /device:TPU:0, one launch (start us, length us, event | category | flops | bytes accessed | tf_op | source)
XLA Modules:
  0.0 146.8 jit_solution(17740853063644884456)
XLA Ops:
  7.2 0.7 iota_add_fusion.1
  7.9 8.9 %all_gather.15 = bf16[128,2048]{1,0:T(8,128)(2,1)S(1)} all-gather(bf16[128,512]{1,0:T(8,128)(2,1)} %param.9), channel_id=1, replica_groups=mesh['replica'=2,'pipe'=4,'tensor'=4] {'tensor'}, dimensions={1}, use_global_device_ids=true | all-gather | bytes 655360 | tf_op jit(solution)/shard_map/all_gather | solution.py:49
  16.9 4.0 %reshape.107 = bf16[4,1024,2,128]{3,2,1,0:T(2,128)(2,1)} reshape(bf16[4,1024,256]{2,1,0:T(8,128)(2,1)} %param.10) | data formatting | bytes 4194304 | tf_op jit(solution)/shard_map/reshape | solution.py:53
  20.9 2.5 %reshape.109 = bf16[4,1024,2,128]{3,2,1,0:T(2,128)(2,1)S(1)} reshape(bf16[4,1024,256]{2,1,0:T(8,128)(2,1)} %param.11) | data formatting | bytes 4194304 | tf_op jit(solution)/shard_map/reshape | solution.py:54
  23.6 3.3 %fusion.3 = (f32[4,32,2,8]{1,3,2,0:T(8,128)S(1)}, f32[4,2,1024,32,8]{2,3,4,1,0:T(8,128)S(1)}) fusion(pred[4,32,1024]{2,1,0:T(8,128)(4,1)S(1)} %broadcast_compare_fusion, bf16[4,32,2,8,128]{4,3,2,1,0:T(8,128)(2,1)S(1)} %bitcast.77, bf16[4,1024,2,128,1]{3,2,1,0,4:T(2,128)(2,1)} %bitcast.75), kind=kOutput, calls=%fused_computation.10 | convolution fusion | flops 543160320 | bytes 11149312 | tf_op jit(solution)/shard_map/rcghd,rjgd->rcghj/dot_general | solution.py:55
  26.9 2.6 %fusion.17 = bf16[4,32,2,8,128]{4,1,3,2,0:T(8,128)(2,1)S(1)} fusion(bf16[4,1024,2,128,1]{3,2,1,0,4:T(2,128)(2,1)S(1)} %bitcast.74, f32[4,2,1024,32,8]{2,3,4,1,0:T(8,128)S(1)} %get-tuple-element.202, f32[4,32,2,8]{1,3,2,0:T(8,128)S(1)} %get-tuple-element.201, pred[4,32,1024]{2,1,0:T(8,128)(4,1)S(1)} %broadcast_compare_fusion), kind=kOutput, calls=%fused_computation.20 | convolution fusion | flops 547618816 | bytes 11149312 | tf_op jit(solution)/shard_map/rcghj,rjgd->rcghd/dot_general | solution.py:66
  29.5 0.6 copy-done
  30.1 1.0 copy.43
  31.3 4.7 %fusion.5 = bf16[4,32,2,8]{1,3,2,0:T(8,128)(2,1)S(1)} fusion(f32[4,2,1024,32,8]{2,3,4,1,0:T(8,128)} %copy-done, f32[4,32,2,8]{1,3,2,0:T(8,128)S(1)} %get-tuple-element.201, pred[4,32,1024]{2,1,0:T(8,128)(4,1)S(1)} %broadcast_compare_fusion), kind=kLoop, calls=%fused_computation.12 | loop fusion | flops 10483712 | bytes 8531968 | tf_op jit(solution)/shard_map/reduce_sum | solution.py:65
  36.1 10.5 %copy.53 = bf16[256,8,4,512]{3,1,2,0:T(8,128)(2,1)} copy(bf16[256,8,4,512]{3,2,1,0:T(4,128)(2,1)} %bitcast.72) | data formatting | bytes 16777216
  46.6 12.3 %copy.45 = bf16[2048,2048]{1,0:T(8,128)(2,1)} copy(bf16[2048,2048]{0,1:T(8,128)(2,1)} %bitcast.71) | data formatting | bytes 16777216 | tf_op jit(solution)/shard_map/dot_general | solution.py:81
  59.0 5.2 %all_gather.17 = bf16[4,128,16]{1,2,0:T(8,128)(2,1)S(1)} all-gather(bf16[1,128,16]{1,2,0:T(8,128)(2,1)S(1)} %convert_element_type.124), channel_id=1, replica_groups=mesh['replica'=2,'pipe'=4,'tensor'=4] {'tensor'}, dimensions={0}, use_global_device_ids=true | all-gather | bytes 20480 | tf_op jit(solution)/shard_map/all_gather | solution.py:15
  64.2 5.4 %all_gather.16 = bf16[4,128,16]{1,2,0:T(8,128)(2,1)S(1)} all-gather(bf16[1,128,16]{1,2,0:T(8,128)(2,1)S(1)} %convert_element_type.120), channel_id=1, replica_groups=mesh['replica'=2,'pipe'=4,'tensor'=4] {'tensor'}, dimensions={0}, use_global_device_ids=true | all-gather | bytes 20480 | tf_op jit(solution)/shard_map/all_gather | solution.py:15
  69.6 1.1 fusion.22
  70.7 6.5 %while.19 = (s32[]{:T(128)}, f32[128,16]{0,1:T(8,128)S(1)}, f32[128,16]{0,1:T(8,128)S(1)}, f32[128,16,128]{2,1,0:T(8,128)S(1)}, bf16[4,128,16]{1,2,0:T(8,128)(2,...) while((s32[]{:T(128)}, f32[128,16]{0,1:T(8,128)S(1)}, ...), condition=%wide.region_3.4_spmd, body=%wide.region_2.3_spmd.sunk | while | flops 1064965 | bytes 2728079 | solution.py:23
  70.9 1.9 %fusion.36 = f32[128,16,128]{2,1,0:T(8,128)S(1)} fusion(f32[128,16,128]{2,1,0:T(8,128)S(1)} %get-tuple-element.267, f32[128,16]{1,0:T(8,128)S(1)} %copy.70, bf16[4,128,16,128]{3,2,1,0:T(8,128)(2,1)} %get-tuple-element.280, s32[]{:T(128)S(6)} %select_n.46, f32[128,16]{1,0:T(8,128)S(1)} %copy.71), kind=kLoop, calls=%fused_computation.1.clone.1 | loop fusion | flops 1048576 | bytes 2637828 | tf_op jit(solution)/shard_map/while/body/eval_jaxpr/add | solution.py:37
  73.1 1.9 %fusion.36 = f32[128,16,128]{2,1,0:T(8,128)S(1)} fusion(f32[128,16,128]{2,1,0:T(8,128)S(1)} %get-tuple-element.267, f32[128,16]{1,0:T(8,128)S(1)} %copy.70, bf16[4,128,16,128]{3,2,1,0:T(8,128)(2,1)} %get-tuple-element.280, s32[]{:T(128)S(6)} %select_n.46, f32[128,16]{1,0:T(8,128)S(1)} %copy.71), kind=kLoop, calls=%fused_computation.1.clone.1 | loop fusion | flops 1048576 | bytes 2637828 | tf_op jit(solution)/shard_map/while/body/eval_jaxpr/add | solution.py:37
  75.3 1.9 %fusion.36 = f32[128,16,128]{2,1,0:T(8,128)S(1)} fusion(f32[128,16,128]{2,1,0:T(8,128)S(1)} %get-tuple-element.267, f32[128,16]{1,0:T(8,128)S(1)} %copy.70, bf16[4,128,16,128]{3,2,1,0:T(8,128)(2,1)} %get-tuple-element.280, s32[]{:T(128)S(6)} %select_n.46, f32[128,16]{1,0:T(8,128)S(1)} %copy.71), kind=kLoop, calls=%fused_computation.1.clone.1 | loop fusion | flops 1048576 | bytes 2637828 | tf_op jit(solution)/shard_map/while/body/eval_jaxpr/add | solution.py:37
  77.4 0.3 divide_convert_fusion
  77.9 7.1 %convolution_convert_fusion = bf16[128,4,512]{2,0,1:T(8,128)(2,1)} fusion(bf16[128,2048,1]{1,0,2:T(8,128)(2,1)S(1)} %reshape.124, bf16[4,512,2048]{2,1,0:T(8,128)(2,1)} %bitcast.70), kind=kOutput, calls=%fused_computation.19 | convolution fusion | flops 1074003968 | bytes 9437184 | tf_op jit(solution)/shard_map/dot_general | solution.py:81
  85.1 22.6 %reduce-scatter.2.cloned.1.call-done = bf16[128,1,512]{2,0,1:T(8,128)(2,1)} async-done(((bf16[128,4,512]{2,0,1:T(8,128)(2,1)}), bf16[128,1,512]{2,0,1:T(8,128)(2,1)}) %reduce-scatter.2.cloned.1.call-update) | async-done | bytes 131088 | tf_op jit(solution)/shard_map/reduce_scatter | solution.py:87
  107.7 1.0 multiply_reduce_fusion
  108.8 29.5 %psum.7 = f32[128]{0:T(128)S(1)} all-reduce(f32[128]{0:T(128)S(1)} %multiply_reduce_fusion), channel_id=1, replica_groups=mesh['replica'=2,'pipe'=4,'tensor'=4] {'pipe','tensor'}, use_global_device_ids=true, to_apply=%region_6.7 | all-reduce | flops 128 | bytes 1024 | tf_op jit(solution)/shard_map/psum | solution.py:97
  138.3 1.7 %multiply_convert_fusion = (bf16[128,512]{1,0:T(8,128)(2,1)}, bf16[128,512]{1,0:T(8,128)(2,1)}) fusion(bf16[128,512]{1,0:T(8,128)(2,1)S(1)} %copy-done.1, bf16[128,1,512]{2,0,1:T(8,128)(2,1)} %reduce-scatter.2.cloned.1.call-done, f32[512]{0:T(512)S(1)} %copy-done.2, f32[128]{0:T(128)S(1)} %add_rsqrt_fusion), kind=kLoop, calls=%fused_computation.26 | loop fusion | flops 458752 | bytes 526848 | tf_op jit(solution)/shard_map/convert_element_type | solution.py:99
  (32 shorter events, 1.6 us)
Async XLA Ops:
  7.2 62.4 %all-gather.2.cloned.1.call-start = ((), (), s32[]{:S(2)}) async-start(), calls=%async_computation.1 | async-start | bytes 2621440 | tf_op jit(solution)/shard_map/all_gather | solution.py:15
  26.9 3.2 %copy-start = (f32[4,2,1024,32,8]{2,3,4,1,0:T(8,128)}, f32[4,2,1024,32,8]{2,3,4,1,0:T(8,128)S(1)}, u32[]{:S(2)}) copy-start(f32[4,2,1024,32,8]{2,3,4,1,0:T(8,128)S(1)} %get-tuple-element.202) | copy-start | bytes 25165828
  31.1 76.6 %reduce-scatter.2.cloned.1.call-start = ((), (), s32[]{:S(2)}) async-start(), calls=%async_computation.2 | async-start | bytes 655360 | tf_op jit(solution)/shard_map/reduce_scatter | solution.py:87
  77.2 30.5 %copy-start.1 = (bf16[128,512]{1,0:T(8,128)(2,1)S(1)}, bf16[128,512]{1,0:T(8,128)(2,1)}, u32[]{:S(2)}) copy-start(bf16[128,512]{1,0:T(8,128)(2,1)} %param.13) | copy-start | bytes 393220
  77.2 61.0 %copy-start.2 = (f32[512]{0:T(512)S(1)}, f32[512]{0:T(512)}, u32[]{:S(2)}) copy-start(f32[512]{0:T(512)} %param.15) | copy-start | bytes 6148
Sparse Core Ops, SparseCore 0:
  31.2 23.3 all-gather.1
  85.2 22.4 reduce-scatter.1
where the time goes:
time: 148 us; the launch traced here: 147 us
  blocking collectives  48.9 us (33%)
  local copies, waits for them, and re-layouts  32.2 us (22%)
  waiting for transfers between devices  22.7 us (15%)
  other arithmetic  15.6 us (11%)
  between operations  14.2 us (10%)
  matrix products  13 us (9%)
    psum x1, blocking collectives, on_device(): squares = lax.psum(jnp.sum(updated * updated, axis=1), ('pipe', 'tensor'))  29.5 us
    reduce_scatter x1, waiting for transfers between devices, on_device(): lax.psum_scatter(partial_value.reshape(tok_rows, col_groups, col_width).a...  22.6 us
    dot_general x1, local copies, waits for them, and re-layouts, on_device(): jnp.dot(attended, out_weight.reshape(out_weight.shape[0], col_groups * co...  12.3 us
    unnamed x8, local copies, waits for them, and re-layouts  11.2 us
    all_gather x2, blocking collectives, combined_all(): lax.all_gather(part.astype(kind), axis)  10.6 us
    all_gather x1, blocking collectives, on_device(): gathered = lax.all_gather(queries, 'tensor', axis=1, tiled=True)  8.87 us
    dot_general x1, matrix products, on_device(): jnp.dot(attended, out_weight.reshape(out_weight.shape[0], col_groups * co...  7.12 us
    add x3, other arithmetic, combine(): summed_one * factor_one[..., None] + summed_two * factor_two[..., None]  5.79 us
  transfers between devices with their start and end apart: 2, of which 1 were waited for; matrix products, arithmetic and copies ran while one was open for 19% of the time, Pallas kernels for 0%

commit v1 on v0

--- a/solution.py
+++ b/solution.py
@@ -8,6 +8,11 @@
 HD = 128
 masked_value = -1e30
 epsilon = 1e-05
+
+
+def gather_and_add(x, mesh_axis):
+    parts = lax.all_gather(x, mesh_axis)
+    return jnp.sum(parts, axis=0)
 
 
 def combined_all(shard, axis, combine):
@@ -94,7 +99,7 @@
         .reshape(tok_rows, col_width)
     )
     updated = residual_in.astype(jnp.float32) + projected
-    squares = lax.psum(jnp.sum(updated * updated, axis=1), ("pipe", "tensor"))
+    squares = gather_and_add(jnp.sum(updated * updated, axis=1), ("pipe", "tensor"))
     normed = updated * lax.rsqrt(squares / D + epsilon)[:, None] * norm_gain[None, :]
     return (updated.astype(jnp.bfloat16), normed.astype(jnp.bfloat16))
 

time: 148 us -> 137 us (0.926)
  blocking collectives: 48.9 us -> 38 us
    psum x1 -> x0, blocking collectives: 29.5 us -> none  [on_device(): squares = lax.psum(jnp.sum(updated * updated, axis=1), ('pipe', 'tensor'))]
    all_gather x0 -> x1, blocking collectives: none -> 18.5 us  [gather_and_add(): parts = lax.all_gather(x, mesh_axis)]
  transfers between devices with their start and end apart: 2 -> 2, of which waited for: 1 -> 1; matrix products, arithmetic and copies ran while one was open for 19% -> 20% of each run, Pallas kernels for 0% -> 0%
where the time goes in v1:
time: 137 us; the launch traced here: 136 us
  blocking collectives  38 us (28%)
  local copies, waits for them, and re-layouts  32.2 us (24%)
  waiting for transfers between devices  22.7 us (17%)
  other arithmetic  15.6 us (11%)
  between operations  14.2 us (10%)
  matrix products  13 us (9%)
    reduce_scatter x1, waiting for transfers between devices, on_device(): lax.psum_scatter(partial_value.reshape(tok_rows, col_groups, col_width).a...  22.6 us
    all_gather x1, blocking collectives, gather_and_add(): parts = lax.all_gather(x, mesh_axis)  18.5 us
    dot_general x1, local copies, waits for them, and re-layouts, on_device(): jnp.dot(attended, out_weight.reshape(out_weight.shape[0], col_groups * co...  12.3 us
    unnamed x8, local copies, waits for them, and re-layouts  11.2 us
    all_gather x2, blocking collectives, combined_all(): lax.all_gather(part.astype(kind), axis)  10.6 us
    all_gather x1, blocking collectives, on_device(): gathered = lax.all_gather(queries, 'tensor', axis=1, tiled=True)  8.87 us
    dot_general x1, matrix products, on_device(): jnp.dot(attended, out_weight.reshape(out_weight.shape[0], col_groups * co...  7.12 us
    add x3, other arithmetic, combine(): summed_one * factor_one[..., None] + summed_two * factor_two[..., None]  5.79 us
  transfers between devices with their start and end apart: 2, of which 1 were waited for; matrix products, arithmetic and copies ran while one was open for 20% of the time, Pallas kernels for 0%

profile of v1, /device:TPU:0, one launch (start us, length us, event | category | flops | bytes accessed | tf_op | source)
XLA Modules:
  0.0 135.8 jit_solution(6000921724019364861)
XLA Ops:
  7.2 0.7 iota_add_fusion.1
  7.9 8.9 %all_gather.21 = bf16[128,2048]{1,0:T(8,128)(2,1)S(1)} all-gather(bf16[128,512]{1,0:T(8,128)(2,1)} %param.9), channel_id=1, replica_groups=mesh['replica'=2,'pipe'=4,'tensor'=4] {'tensor'}, dimensions={1}, use_global_device_ids=true | all-gather | bytes 655360 | tf_op jit(solution)/shard_map/all_gather | solution.py:54
  16.9 4.0 %reshape.111 = bf16[4,1024,2,128]{3,2,1,0:T(2,128)(2,1)} reshape(bf16[4,1024,256]{2,1,0:T(8,128)(2,1)} %param.10) | data formatting | bytes 4194304 | tf_op jit(solution)/shard_map/reshape | solution.py:58
  20.9 2.5 %reshape.113 = bf16[4,1024,2,128]{3,2,1,0:T(2,128)(2,1)S(1)} reshape(bf16[4,1024,256]{2,1,0:T(8,128)(2,1)} %param.11) | data formatting | bytes 4194304 | tf_op jit(solution)/shard_map/reshape | solution.py:59
  23.6 3.3 %fusion.3 = (f32[4,32,2,8]{1,3,2,0:T(8,128)S(1)}, f32[4,2,1024,32,8]{2,3,4,1,0:T(8,128)S(1)}) fusion(pred[4,32,1024]{2,1,0:T(8,128)(4,1)S(1)} %broadcast_compare_fusion, bf16[4,32,2,8,128]{4,3,2,1,0:T(8,128)(2,1)S(1)} %bitcast.78, bf16[4,1024,2,128,1]{3,2,1,0,4:T(2,128)(2,1)} %bitcast.76), kind=kOutput, calls=%fused_computation.10 | convolution fusion | flops 543160320 | bytes 11149312 | tf_op jit(solution)/shard_map/rcghd,rjgd->rcghj/dot_general | solution.py:60
  26.9 2.6 %fusion.17 = bf16[4,32,2,8,128]{4,1,3,2,0:T(8,128)(2,1)S(1)} fusion(bf16[4,1024,2,128,1]{3,2,1,0,4:T(2,128)(2,1)S(1)} %bitcast.75, f32[4,2,1024,32,8]{2,3,4,1,0:T(8,128)S(1)} %get-tuple-element.202, f32[4,32,2,8]{1,3,2,0:T(8,128)S(1)} %get-tuple-element.201, pred[4,32,1024]{2,1,0:T(8,128)(4,1)S(1)} %broadcast_compare_fusion), kind=kOutput, calls=%fused_computation.20 | convolution fusion | flops 547618816 | bytes 11149312 | tf_op jit(solution)/shard_map/rcghj,rjgd->rcghd/dot_general | solution.py:71
  29.5 0.6 copy-done
  30.1 1.0 copy.43
  31.3 4.7 %fusion.5 = bf16[4,32,2,8]{1,3,2,0:T(8,128)(2,1)S(1)} fusion(f32[4,2,1024,32,8]{2,3,4,1,0:T(8,128)} %copy-done, f32[4,32,2,8]{1,3,2,0:T(8,128)S(1)} %get-tuple-element.201, pred[4,32,1024]{2,1,0:T(8,128)(4,1)S(1)} %broadcast_compare_fusion), kind=kLoop, calls=%fused_computation.12 | loop fusion | flops 10483712 | bytes 8531968 | tf_op jit(solution)/shard_map/reduce_sum | solution.py:70
  36.1 10.5 %copy.53 = bf16[256,8,4,512]{3,1,2,0:T(8,128)(2,1)} copy(bf16[256,8,4,512]{3,2,1,0:T(4,128)(2,1)} %bitcast.73) | data formatting | bytes 16777216
  46.6 12.3 %copy.45 = bf16[2048,2048]{1,0:T(8,128)(2,1)} copy(bf16[2048,2048]{0,1:T(8,128)(2,1)} %bitcast.72) | data formatting | bytes 16777216 | tf_op jit(solution)/shard_map/dot_general | solution.py:86
  59.0 5.2 %all_gather.23 = bf16[4,128,16]{1,2,0:T(8,128)(2,1)S(1)} all-gather(bf16[1,128,16]{1,2,0:T(8,128)(2,1)S(1)} %convert_element_type.124), channel_id=1, replica_groups=mesh['replica'=2,'pipe'=4,'tensor'=4] {'tensor'}, dimensions={0}, use_global_device_ids=true | all-gather | bytes 20480 | tf_op jit(solution)/shard_map/all_gather | solution.py:20
  64.2 5.4 %all_gather.22 = bf16[4,128,16]{1,2,0:T(8,128)(2,1)S(1)} all-gather(bf16[1,128,16]{1,2,0:T(8,128)(2,1)S(1)} %convert_element_type.120), channel_id=1, replica_groups=mesh['replica'=2,'pipe'=4,'tensor'=4] {'tensor'}, dimensions={0}, use_global_device_ids=true | all-gather | bytes 20480 | tf_op jit(solution)/shard_map/all_gather | solution.py:20
  69.6 1.1 fusion.22
  70.7 6.5 %while.19 = (s32[]{:T(128)}, f32[128,16]{0,1:T(8,128)S(1)}, f32[128,16]{0,1:T(8,128)S(1)}, f32[128,16,128]{2,1,0:T(8,128)S(1)}, bf16[4,128,16]{1,2,0:T(8,128)(2,...) while((s32[]{:T(128)}, f32[128,16]{0,1:T(8,128)S(1)}, ...), condition=%wide.region_3.4_spmd, body=%wide.region_2.3_spmd.sunk | while | flops 1064965 | bytes 2728079 | solution.py:28
  70.9 1.9 %fusion.36 = f32[128,16,128]{2,1,0:T(8,128)S(1)} fusion(f32[128,16,128]{2,1,0:T(8,128)S(1)} %get-tuple-element.267, f32[128,16]{1,0:T(8,128)S(1)} %copy.70, bf16[4,128,16,128]{3,2,1,0:T(8,128)(2,1)} %get-tuple-element.280, s32[]{:T(128)S(6)} %select_n.46, f32[128,16]{1,0:T(8,128)S(1)} %copy.71), kind=kLoop, calls=%fused_computation.1.clone.1 | loop fusion | flops 1048576 | bytes 2637828 | tf_op jit(solution)/shard_map/while/body/eval_jaxpr/add | solution.py:42
  73.1 1.9 %fusion.36 = f32[128,16,128]{2,1,0:T(8,128)S(1)} fusion(f32[128,16,128]{2,1,0:T(8,128)S(1)} %get-tuple-element.267, f32[128,16]{1,0:T(8,128)S(1)} %copy.70, bf16[4,128,16,128]{3,2,1,0:T(8,128)(2,1)} %get-tuple-element.280, s32[]{:T(128)S(6)} %select_n.46, f32[128,16]{1,0:T(8,128)S(1)} %copy.71), kind=kLoop, calls=%fused_computation.1.clone.1 | loop fusion | flops 1048576 | bytes 2637828 | tf_op jit(solution)/shard_map/while/body/eval_jaxpr/add | solution.py:42
  75.3 1.9 %fusion.36 = f32[128,16,128]{2,1,0:T(8,128)S(1)} fusion(f32[128,16,128]{2,1,0:T(8,128)S(1)} %get-tuple-element.267, f32[128,16]{1,0:T(8,128)S(1)} %copy.70, bf16[4,128,16,128]{3,2,1,0:T(8,128)(2,1)} %get-tuple-element.280, s32[]{:T(128)S(6)} %select_n.46, f32[128,16]{1,0:T(8,128)S(1)} %copy.71), kind=kLoop, calls=%fused_computation.1.clone.1 | loop fusion | flops 1048576 | bytes 2637828 | tf_op jit(solution)/shard_map/while/body/eval_jaxpr/add | solution.py:42
  77.4 0.3 divide_convert_fusion
  77.9 7.1 %convolution_convert_fusion = bf16[128,4,512]{2,0,1:T(8,128)(2,1)} fusion(bf16[128,2048,1]{1,0,2:T(8,128)(2,1)S(1)} %reshape.132, bf16[4,512,2048]{2,1,0:T(8,128)(2,1)} %bitcast.71), kind=kOutput, calls=%fused_computation.19 | convolution fusion | flops 1074003968 | bytes 9437184 | tf_op jit(solution)/shard_map/dot_general | solution.py:86
  85.1 22.6 %reduce-scatter.2.cloned.1.call-done = bf16[128,1,512]{2,0,1:T(8,128)(2,1)} async-done(((bf16[128,4,512]{2,0,1:T(8,128)(2,1)}), bf16[128,1,512]{2,0,1:T(8,128)(2,1)}) %reduce-scatter.2.cloned.1.call-update) | async-done | bytes 131088 | tf_op jit(solution)/shard_map/reduce_scatter | solution.py:92
  107.7 1.0 multiply_reduce_fusion
  108.8 18.5 %all-gather.1 = f32[16,1,128]{2,1,0:T(1,128)S(1)} all-gather(f32[1,1,128]{2,1,0:T(1,128)S(1)} %bitcast.79), channel_id=2, replica_groups=mesh['replica'=2,'pipe'=4,'tensor'=4] {'pipe','tensor'}, dimensions={0}, use_global_device_ids=true | all-gather | bytes 8704 | tf_op jit(solution)/shard_map/all_gather | solution.py:14
  127.3 1.7 %multiply_convert_fusion = (bf16[128,512]{1,0:T(8,128)(2,1)}, bf16[128,512]{1,0:T(8,128)(2,1)}) fusion(bf16[128,512]{1,0:T(8,128)(2,1)S(1)} %copy-done.1, bf16[128,1,512]{2,0,1:T(8,128)(2,1)} %reduce-scatter.2.cloned.1.call-done, f32[512]{0:T(512)S(1)} %copy-done.2, f32[128]{0:T(128)S(1)} %add_rsqrt_fusion), kind=kLoop, calls=%fused_computation.26 | loop fusion | flops 458752 | bytes 526848 | tf_op jit(solution)/shard_map/convert_element_type | solution.py:104
  (33 shorter events, 1.6 us)
Async XLA Ops:
  7.2 62.4 %all-gather.4.cloned.1.call-start = ((), (), s32[]{:S(2)}) async-start(), calls=%async_computation.1 | async-start | bytes 2621440 | tf_op jit(solution)/shard_map/all_gather | solution.py:20
  26.9 3.2 %copy-start = (f32[4,2,1024,32,8]{2,3,4,1,0:T(8,128)}, f32[4,2,1024,32,8]{2,3,4,1,0:T(8,128)S(1)}, u32[]{:S(2)}) copy-start(f32[4,2,1024,32,8]{2,3,4,1,0:T(8,128)S(1)} %get-tuple-element.202) | copy-start | bytes 25165828
  31.1 76.6 %reduce-scatter.2.cloned.1.call-start = ((), (), s32[]{:S(2)}) async-start(), calls=%async_computation.2 | async-start | bytes 655360 | tf_op jit(solution)/shard_map/reduce_scatter | solution.py:92
  77.2 30.5 %copy-start.1 = (bf16[128,512]{1,0:T(8,128)(2,1)S(1)}, bf16[128,512]{1,0:T(8,128)(2,1)}, u32[]{:S(2)}) copy-start(bf16[128,512]{1,0:T(8,128)(2,1)} %param.13) | copy-start | bytes 393220
  77.2 50.1 %copy-start.2 = (f32[512]{0:T(512)S(1)}, f32[512]{0:T(512)}, u32[]{:S(2)}) copy-start(f32[512]{0:T(512)} %param.15) | copy-start | bytes 6148
Sparse Core Ops, SparseCore 0:
  31.2 23.3 all-gather.3
  85.2 22.4 reduce-scatter.1
